TPU v7x, 32 devices: a whole 2x2x4 slice. The times are simulated.
32 devices in a mesh: chan: 4 (over x, core), bl: 8 (over z, y).
Axes of the slice: x: 2, y: 2, z: 4, core: 2. Of those that a mesh axis runs over, the one named last changes fastest.
Arguments:
- vis_value: bfloat16 [4, 8, 2, 2048], P('chan', 'bl'), may hold values from -6 to 6
- vis_weight: bfloat16 [4, 8, 2048], P('chan', 'bl'), may hold values from 0.19921875 to 5
- kernel: bfloat16 [4, 8, 64, 2048], P('chan', 'bl'), may hold values from 0.049804688 to 1
- tile_index: int32 [4, 8, 2048], P('chan', 'bl'), may hold values from 0 to 262143
- plane_index: int32 [4, 8, 2048], P('chan', 'bl'), may hold values from 0 to 7
- chan_index: int32 [4, 8, 2048], P('chan', 'bl'), may hold values from 0 to 15
- chan_offset: float32 [4, 16], P('chan'), may hold values from -0.4 to 0.4
- counts: int32 [4, 8], P('chan', 'bl'), may hold values from 256 to 2048, as said below
Outputs:
- taylor_coeffs: float32 [3, 32768], P(None, ('chan', 'bl'))
Inputs may be any that keep to these rules, and one draw needn't show every extreme that they name: `counts`: each device's number of live visibility slots; slots from that number on are ignored. In every draw some device has exactly 2048.
All inputs are finite; a program needn't handle non-finite values.
Results may differ from a plain program's by a relative error of at most 0.0003.
Values may be sent and summed in bfloat16 or wider, within the bound.
A program may use at most 128 MiB of HBM per device.

v0:
```python
import functools

import numpy as np
import jax
import jax.numpy as jnp
from jax import lax
from jax.experimental import pallas as pl
from jax.experimental.pallas import tpu as pltpu
from jax.sharding import PartitionSpec as P

NPIX = 4096
TILE = 8
TAYLOR = 3
MOMENTS = 5
WPLANES = 8
STRIP = 8
BLK = 256
LANES = 128

two_pi = 2.0 * np.pi
w_step = 40.0
ntiles = NPIX // TILE
radix = 256
fine = NPIX // radix
half = fine * STRIP
MESH = pl.DeviceIdType.MESH


def split(x):
    high = x.astype(jnp.bfloat16)
    low = (x - high.astype(jnp.float32)).astype(jnp.bfloat16)
    return high, low


@functools.cache
def tables():
    f32 = np.float32
    bf16 = jnp.bfloat16

    def two(x):
        x = x.astype(f32)
        high = x.astype(bf16)
        return high, (x - high.astype(f32)).astype(bf16)

    rows = np.arange(STRIP) - STRIP // 2
    taps = np.zeros((2, TILE, STRIP, TILE, TILE))
    angle = two_pi * np.arange(TILE)[:, None] * rows[None, :] / NPIX
    for e in range(TILE):
        taps[0, e, :, :, e] = np.cos(angle).T
        taps[1, e, :, :, e] = np.sin(angle).T
    tap_high, tap_low = two(taps.reshape(2 * TILE * STRIP, TILE * TILE))
    tap_table = np.concatenate([tap_high, tap_low], axis=1)
    ids = np.arange(radix)
    angle = two_pi * (ids[:, None] * ids[None, :] % radix) / radix
    coarse_high, coarse_low = two(np.concatenate([np.cos(angle), np.sin(angle)], axis=1))
    coarse = np.concatenate([coarse_high, coarse_low], axis=0)
    cells = np.arange(fine)
    angle = two_pi * cells[:, None] * ids[None, :] / NPIX
    sign = 1.0 - 2.0 * ((cells[:, None] + ids[None, :]) % 2)
    twist = np.stack([np.cos(angle) * sign, np.sin(angle) * sign])
    twist = np.repeat(twist, STRIP, axis=1).astype(f32)
    angle = two_pi * (cells[:, None] * cells[None, :] % fine) / fine
    eye = np.eye(STRIP)
    cosine = np.einsum("me,lL->lmeL", np.cos(angle), eye).reshape(half, half)
    sine = np.einsum("me,lL->lmeL", np.sin(angle), eye).reshape(half, half)
    fine_high, fine_low = two(np.block([[cosine, -sine], [sine, cosine]]))
    fine_table = np.concatenate([fine_high, fine_low, fine_high], axis=1)
    cell_size = 0.5 / NPIX
    x = rows * cell_size
    y = (np.arange(NPIX) - NPIX // 2) * cell_size
    radius = x[:, None] ** 2 + y[None, :] ** 2
    lowered = -radius / (1.0 + np.sqrt(1.0 - radius))
    w = w_step * (np.arange(WPLANES // 2) - 0.5 * (WPLANES - 1))
    angle = two_pi * w[:, None, None] * lowered[None]
    angle = angle.reshape(WPLANES // 2, STRIP * fine, radix)
    screen = np.stack([np.cos(angle), np.sin(angle)], axis=1).astype(f32)
    return tap_table, coarse, twist, fine_table, screen


def image_kernel(
    count_ref, offset_ref, value_ref, weight_ref, kernel_ref, tile_ref, plane_ref, chan_ref,
    tap_ref, coarse_hbm, twist_hbm, fine_hbm, screen_hbm,
    image_ref, moment_ref, coarse_ref, twist_ref, fine_ref, screen_ref, grid_ref, upd_ref, mom_ref, turn_ref, flat_ref, sems,
):
    loads = [
        pltpu.make_async_copy(source, target, sems.at[i])
        for i, (source, target) in enumerate((
            (coarse_hbm, coarse_ref), (twist_hbm, twist_ref),
            (fine_hbm, fine_ref), (screen_hbm, screen_ref),
        ))
    ]
    for load in loads:
        load.start()
    count = count_ref[0, 0]
    grid_ref[...] = jnp.zeros_like(grid_ref)
    mom_ref[...] = jnp.zeros_like(mom_ref)

    def one_block(block, carry):
        first = pl.multiple_of(block * BLK, BLK)
        here = pl.ds(first, BLK)
        slot = first + lax.broadcasted_iota(jnp.int32, (1, BLK), 1)
        tiles = tile_ref[:, here]
        planes = plane_ref[:, here]
        chans = chan_ref[:, here]
        coord = jnp.zeros((1, BLK), jnp.float32)
        for c in range(offset_ref.shape[1]):
            coord = jnp.where(chans == c, offset_ref[0, c], coord)
        weight = weight_ref[0:1, here].astype(jnp.float32)
        weight = jnp.where(slot < count, weight, 0.0)
        taps = kernel_ref[:, here]
        value = value_ref[:, here].astype(jnp.float32)
        base_real = weight * value[0:1]
        base_imag = weight * value[1:2]

        u_tile = lax.shift_right_logical(tiles, 9)
        v_tile = tiles & (ntiles - 1)
        strip = lax.broadcasted_iota(jnp.int32, (STRIP, BLK), 0) - STRIP // 2
        phase = ((u_tile - ntiles // 2) * strip) & (ntiles - 1)
        angle = phase.astype(jnp.float32) * (two_pi / ntiles)
        cosine = jnp.cos(angle)
        sine = jnp.sin(angle)
        z_real = base_real * cosine - base_imag * sine
        z_imag = base_real * sine + base_imag * cosine

        sums = jnp.dot(
            tap_ref[...], jnp.concatenate([taps, taps], axis=0),
            preferred_element_type=jnp.float32,
        )
        sum_real = sums[: TILE * STRIP].reshape(TILE, STRIP, BLK)
        sum_imag = sums[TILE * STRIP :].reshape(TILE, STRIP, BLK)
        part_real = (sum_real * z_real[None] - sum_imag * z_imag[None]).reshape(-1, BLK)
        part_imag = (sum_real * z_imag[None] + sum_imag * z_real[None]).reshape(-1, BLK)
        odd = (v_tile & 1).astype(jnp.float32)
        even = 1.0 - odd
        for k in range(TAYLOR):
            for c, part in enumerate((part_real, part_imag)):
                for side, mask in enumerate((even, odd)):
                    high, low = split(part * mask)
                    row = (k * 2 + c) * half + side * (half // 2)
                    upd_ref[row : row + half // 2, :BLK] = high
                    upd_ref[row : row + half // 2, BLK:] = low
            if k + 1 < TAYLOR:
                part_real = part_real * coord
                part_imag = part_imag * coord

        weighted = weight * jnp.sum(taps.astype(jnp.float32), axis=0, keepdims=True)
        for m in range(MOMENTS):
            mom_ref[m : m + 1, :] += weighted
            weighted = weighted * coord

        target = planes * radix + lax.shift_right_logical(v_tile, 1)
        column = jnp.transpose(jnp.broadcast_to(target.astype(jnp.float32), (LANES, BLK)))
        column = jnp.concatenate([column, column], axis=1)
        update = upd_ref[...]
        lane = lax.broadcasted_iota(jnp.int32, (BLK, radix), 1).astype(jnp.float32)
        for p in range(WPLANES):
            hot = jnp.where(column == lane + float(p * radix), 1.0, 0.0).astype(jnp.bfloat16)
            grid_ref[p] += jnp.dot(
                update[:, :BLK], hot, preferred_element_type=jnp.float32
            ) + jnp.dot(update[:, BLK:], hot, preferred_element_type=jnp.float32)
        return carry

    lax.fori_loop(0, (count + BLK - 1) // BLK, one_block, 0)
    moment_ref[...] = jnp.broadcast_to(
        jnp.sum(mom_ref[...], axis=1, keepdims=True), moment_ref.shape
    )

    for load in loads:
        load.wait()
    coarse_high = coarse_ref[:radix]
    coarse_table = jnp.concatenate([coarse_high, coarse_ref[radix:], coarse_high], axis=0)
    turn_ref[...] = jnp.zeros_like(turn_ref)

    def one_plane(p, carry):
        high, low = split(grid_ref[p])
        spectra = jnp.dot(
            jnp.concatenate([high, high, low], axis=1), coarse_table,
            preferred_element_type=jnp.float32,
        )
        mirror = jnp.minimum(p, WPLANES - 1 - p)
        sign = jnp.where(p < WPLANES // 2, 1.0, -1.0)
        screen_real = screen_ref[mirror, 0]
        screen_imag = screen_ref[mirror, 1] * sign
        for k in range(TAYLOR):
            real = spectra[2 * k * half : (2 * k + 1) * half]
            imag = spectra[(2 * k + 1) * half : (2 * k + 2) * half]
            f_real = real[:, :radix] - imag[:, radix:]
            f_imag = imag[:, :radix] + real[:, radix:]
            x_real = f_real * twist_ref[0] - f_imag * twist_ref[1]
            x_imag = f_real * twist_ref[1] + f_imag * twist_ref[0]
            x_high, x_low = split(jnp.concatenate([x_real, x_imag], axis=0))
            y = jnp.dot(
                fine_ref[...], jnp.concatenate([x_high, x_high, x_low], axis=0),
                preferred_element_type=jnp.float32,
            )
            turn_ref[k] += y[:half] * screen_real - y[half:] * screen_imag
        return carry

    lax.fori_loop(0, WPLANES, one_plane, 0)
    pieces = radix // LANES
    chunks, _, rows, _ = image_ref.shape
    for k in range(TAYLOR):
        for h in range(pieces):
            flat_ref[pl.ds(h, half, stride=pieces), :] = turn_ref[k, :, h * LANES : (h + 1) * LANES]
        image_ref[:, k] = flat_ref[...].reshape(chunks, rows, LANES)


def local_image(chunks, count, offsets, value, weight, kernel, tiles, planes, chans):
    rows = STRIP * NPIX // (chunks * LANES)
    consts = [jnp.asarray(t) for t in tables()]
    smem = pl.BlockSpec(memory_space=pltpu.SMEM)
    vmem = pl.BlockSpec(memory_space=pltpu.VMEM)
    hbm = pl.BlockSpec(memory_space=pl.ANY)
    columns = 2 * TAYLOR * half
    return pl.pallas_call(
        image_kernel,
        out_shape=(
            jax.ShapeDtypeStruct((chunks, TAYLOR, rows, LANES), jnp.float32),
            jax.ShapeDtypeStruct((8, LANES), jnp.float32),
        ),
        in_specs=[smem, smem] + [vmem] * 7 + [hbm] * 4,
        out_specs=(vmem, vmem),
        scratch_shapes=[pltpu.VMEM(c.shape, c.dtype) for c in consts[1:]]
        + [
            pltpu.VMEM((WPLANES, columns, radix), jnp.float32),
            pltpu.VMEM((columns, 2 * BLK), jnp.bfloat16),
            pltpu.VMEM((8, BLK), jnp.float32),
            pltpu.VMEM((TAYLOR, half, radix), jnp.float32),
            pltpu.VMEM((half * radix // LANES, LANES), jnp.float32),
            pltpu.SemaphoreType.DMA((4,)),
        ],
        compiler_params=pltpu.CompilerParams(vmem_limit_bytes=56 * 1024 * 1024),
        name="local_image",
    )(count, offsets, value, weight, kernel, tiles, planes, chans, *consts)


def solve_taylor(moments, images):
    entry_00, entry_01, entry_02 = (moments[0], moments[1], moments[2])
    entry_11, entry_12, entry_22 = (moments[2], moments[3], moments[4])
    minor_00 = entry_11 * entry_22 - entry_12 * entry_12
    minor_01 = entry_02 * entry_12 - entry_01 * entry_22
    minor_02 = entry_01 * entry_12 - entry_02 * entry_11
    minor_11 = entry_00 * entry_22 - entry_02 * entry_02
    minor_12 = entry_01 * entry_02 - entry_00 * entry_12
    minor_22 = entry_00 * entry_11 - entry_01 * entry_01
    determinant = entry_00 * minor_00 + entry_01 * minor_01 + entry_02 * minor_02
    first = (minor_00 * images[0] + minor_01 * images[1] + minor_02 * images[2]) / determinant
    second = (minor_01 * images[0] + minor_11 * images[1] + minor_12 * images[2]) / determinant
    third = (minor_02 * images[0] + minor_12 * images[1] + minor_22 * images[2]) / determinant
    return first, second, third


def reduce_kernel(
    n_chan, n_bl, image_ref, moment_ref, out_ref,
    work_ref, land_ref, sum_ref, mom_send_ref, mom_land_ref, bl_land_ref, bl_mom_ref,
    send_sem, recv_sem, mom_send_sem, mom_recv_sem, bl_send, bl_recv, blm_send, blm_recv,
):
    chan = lax.axis_index("chan")
    bl = lax.axis_index("bl")
    steps = n_chan.bit_length() - 1

    def partner(s):
        return chan + (1 - 2 * ((chan // 2**s) % 2)) * 2**s

    def peer(d):
        return lax.rem(bl + d, n_bl)

    barrier = pltpu.get_barrier_semaphore()
    for s in range(steps):
        pl.semaphore_signal(barrier, inc=1, device_id=(partner(s), bl), device_id_type=MESH)
    for d in range(1, n_bl):
        pl.semaphore_signal(barrier, inc=1, device_id=(chan, peer(d)), device_id_type=MESH)
    pl.semaphore_wait(barrier, steps + n_bl - 1)

    slot = 0
    for s in range(steps):
        stride = 2 ** (s + 1)
        pieces = n_chan // stride
        copies = [
            pltpu.make_async_remote_copy(
                src_ref=moment_ref if s == 0 else mom_send_ref.at[s],
                dst_ref=mom_land_ref.at[s],
                send_sem=mom_send_sem.at[s], recv_sem=mom_recv_sem.at[s],
                device_id=(partner(s), bl), device_id_type=MESH,
            )
        ]
        for i in range(pieces):
            if s == 0:
                source = image_ref.at[partner(0) % 2 + i * 2]
            else:
                source = work_ref.at[s - 1, (partner(s) // 2**s) % 2 + 2 * i]
            copies.append(
                pltpu.make_async_remote_copy(
                    src_ref=source, dst_ref=land_ref.at[slot + i],
                    send_sem=send_sem.at[slot + i], recv_sem=recv_sem.at[slot + i],
                    device_id=(partner(s), bl), device_id_type=MESH,
                )
            )
        for copy in copies:
            copy.start()
        copies[0].wait()
        before = moment_ref[...] if s == 0 else mom_send_ref[s]
        mom_send_ref[s + 1] = before + mom_land_ref[s]
        for i in range(pieces):
            copies[1 + i].wait()
            if s == 0:
                own = image_ref[chan % 2 + i * 2]
            else:
                own = work_ref[s - 1, (chan // 2**s) % 2 + 2 * i]
            if s + 1 < steps:
                work_ref[s, i] = own + land_ref[slot + i]
            else:
                sum_ref[...] = own + land_ref[slot + i]
        slot += pieces

    copies = []
    for d in range(1, n_bl):
        copies.append(
            pltpu.make_async_remote_copy(
                src_ref=mom_send_ref.at[steps], dst_ref=bl_mom_ref.at[d],
                send_sem=blm_send.at[d], recv_sem=blm_recv.at[d],
                device_id=(chan, peer(d)), device_id_type=MESH,
            )
        )
        copies.append(
            pltpu.make_async_remote_copy(
                src_ref=sum_ref.at[peer(d)], dst_ref=bl_land_ref.at[d],
                send_sem=bl_send.at[d], recv_sem=bl_recv.at[d],
                device_id=(chan, peer(d)), device_id_type=MESH,
            )
        )
    for copy in copies:
        copy.start()
    moments = mom_send_ref[steps]
    images = sum_ref[bl]
    for d in range(1, n_bl):
        copies[2 * d - 2].wait()
        copies[2 * d - 1].wait()
        moments = moments + bl_mom_ref[d]
        images = images + bl_land_ref[d]
    solved = solve_taylor([moments[m : m + 1] for m in range(MOMENTS)], images)
    for k in range(TAYLOR):
        out_ref[k] = solved[k]


def reduce_solve(n_chan, n_bl, image, moment):
    chunks, taylor, rows, lanes = image.shape
    image = image.reshape(n_chan, n_bl, taylor, rows, lanes)
    vmem = pl.BlockSpec(memory_space=pltpu.VMEM)
    block = (n_bl, taylor, rows, lanes)
    steps = n_chan.bit_length() - 1
    dma = pltpu.SemaphoreType.DMA
    return pl.pallas_call(
        functools.partial(reduce_kernel, n_chan, n_bl),
        out_shape=jax.ShapeDtypeStruct((taylor, rows, lanes), jnp.float32),
        in_specs=[vmem, vmem],
        out_specs=vmem,
        scratch_shapes=[
            pltpu.VMEM((max(steps - 1, 1), n_chan // 2) + block, jnp.float32),
            pltpu.VMEM((n_chan - 1,) + block, jnp.float32),
            pltpu.VMEM(block, jnp.float32),
            pltpu.VMEM((steps + 1, 8, lanes), jnp.float32),
            pltpu.VMEM((steps, 8, lanes), jnp.float32),
            pltpu.VMEM((n_bl, taylor, rows, lanes), jnp.float32),
            pltpu.VMEM((n_bl, 8, lanes), jnp.float32),
            dma((n_chan - 1,)), dma((n_chan - 1,)), dma((steps,)), dma((steps,)),
            dma((n_bl,)), dma((n_bl,)), dma((n_bl,)), dma((n_bl,)),
        ],
        compiler_params=pltpu.CompilerParams(collective_id=0, has_side_effects=True),
        name="reduce_solve",
    )(image, moment)


def solution(mesh):
    n_chan = mesh.shape["chan"]
    n_bl = mesh.shape["bl"]

    def body(vis_value, vis_weight, kernel, tile_index, plane_index, chan_index, chan_offset, counts):
        image, moment = local_image(
            n_chan * n_bl, counts, chan_offset, vis_value[0, 0], vis_weight[0], kernel[0, 0],
            tile_index[0], plane_index[0], chan_index[0],
        )
        out = reduce_solve(n_chan, n_bl, image, moment)
        return out.reshape(TAYLOR, -1)

    in_specs = (
        P("chan", "bl", None, None),
        P("chan", "bl", None),
        P("chan", "bl", None, None),
        P("chan", "bl", None),
        P("chan", "bl", None),
        P("chan", "bl", None),
        P("chan", None),
        P("chan", "bl"),
    )
    out_specs = P(None, ("chan", "bl"))
    return jax.shard_map(body, mesh=mesh, in_specs=in_specs, out_specs=out_specs, check_vma=False)
```

profile of v0, /device:TPU:0, one launch (start us, length us, event | category | flops | bytes accessed | tf_op | source)
XLA Modules:
  0.0 51.6 jit_solution(15236456449960896813)
XLA Ops:
  0.7 20.3 %local_image.1 = (f32[32,3,8,128]{3,2,1,0:T(8,128)}, f32[8,128]{1,0:T(8,128)}) custom-call(s32[1,1]{1,0:T(1,128)S(6)} %copy.17.count_ref, f32[1,16]{1,0:T(1,128)} %offset_ref.1, bf16[2,2048]{1,0:T(2,128)(2,1)} %bitcast.14, bf16[1,2048]{1,0:T(2,128)(2,1)} %bitcast.15, bf16[64,2048]{1,0:T(8,128)(2,1)} %bitcast.12, s32[1,2048]{1,0:T(1,128)} %bitcast.16, ...), custom_call_target="tpu_custom_call" | custom-call | tf_op jit(solution)/shard_map/local_image/pallas_call | solution.py:215
  21.0 29.3 %reduce_solve.1 = f32[3,8,128]{2,1,0:T(8,128)} custom-call(f32[4,8,3,8,128]{4,3,2,1,0:T(8,128)} %bitcast.11, f32[8,128]{1,0:T(8,128)} %get-tuple-element.8.moment_ref), custom_call_target="tpu_custom_call" | custom-call | tf_op jit(solution)/shard_map/reduce_solve/pallas_call | solution.py:353
  50.3 1.3 %copy.16 = f32[1,3,8,128]{3,1,2,0:T(4,128)} copy(f32[1,3,8,128]{3,2,1,0:T(8,128)} %bitcast.13) | data formatting | bytes 24576
where the time goes:
time: 51.7 us; the launch traced here: 51.6 us
  Pallas kernels  49.6 us (96%)
  local copies, waits for them, and re-layouts  1.32 us (3%)
  between operations  0.67 us (1%)
    pallas_call x1, Pallas kernels, reduce_solve(): pl.pallas_call(functools.partial(reduce_kernel, n_chan, n_bl), out_shape=...  29.3 us
    pallas_call x1, Pallas kernels, local_image(): pl.pallas_call(image_kernel, out_shape=(jax.ShapeDtypeStruct((chunks, TAY...  20.3 us
    unnamed x1, local copies, waits for them, and re-layouts  1.32 us

commit v1 on v0

v1 whole, which is shorter than its diff:
```python
import functools

import numpy as np
import jax
import jax.numpy as jnp
from jax import lax
from jax.experimental import pallas as pl
from jax.experimental.pallas import tpu as pltpu
from jax.sharding import PartitionSpec as P

NPIX = 4096
TILE = 8
TAYLOR = 3
MOMENTS = 5
WPLANES = 8
STRIP = 8
LANES = 128
CORES = 2

two_pi = 2.0 * np.pi
w_step = 40.0
ntiles = NPIX // TILE
planes = WPLANES // 2
held = STRIP // CORES
quads = ntiles // LANES
groups = planes * quads // 2
pairs = TILE // 2
per_k = TILE * STRIP + 8
rows_all = TAYLOR * per_k
BLK = 512
MESH = pl.DeviceIdType.MESH


def split(x):
    high = x.astype(jnp.bfloat16)
    low = (x - high.astype(jnp.float32)).astype(jnp.bfloat16)
    return high, low


def cosine_series():
    g = 0.125 - 0.125 * np.cos(np.pi * (np.arange(64) + 0.5) / 64)
    fit = np.polynomial.Polynomial.fit(g, np.cos(two_pi * np.sqrt(g)), 8, domain=[0.0, 0.25])
    return [float(c) for c in fit.convert().coef]


cos_terms = cosine_series()


@functools.cache
def tables(n_chan):
    f32 = np.float32
    bf16 = jnp.bfloat16
    per = STRIP // n_chan

    def two(x):
        x = x.astype(f32)
        high = x.astype(bf16)
        return high, (x - high.astype(f32)).astype(bf16)

    slot = np.arange(held)
    strips = [(slot // per * CORES + core) * per + slot % per for core in range(CORES)]
    sub_e = np.arange(8) // held
    sub_l = np.arange(8) % held

    taps = np.zeros((CORES, 88, 2, TILE, TILE))
    for core in range(CORES):
        offset = strips[core] - STRIP // 2
        angle = two_pi * np.arange(TILE)[None, :] * offset[:, None] / NPIX
        for e in range(TILE + 1):
            for part, wave in enumerate((np.cos(angle), np.sin(angle))):
                if e < TILE:
                    rows = [part * 32 + e // 2 * 8 + e % 2 * held + slot]
                else:
                    rows = [64 + part * 8 + slot, 64 + part * 8 + held + slot]
                for row in rows:
                    if e < TILE:
                        taps[core, row, 0, :, e] = wave
                    if e > 0:
                        taps[core, row, 1, :, TILE - e] = wave
    taps[:, 80:] = 1.0
    tap_high, tap_low = two(taps.reshape(CORES, 88, 2 * TILE * TILE))
    tap_table = np.concatenate([tap_high, tap_low], axis=2)

    ids = np.arange(LANES)
    angle = two_pi * (ids[:, None] * ids[None, :] % LANES) / LANES
    cosine, sine = np.cos(angle), np.sin(angle)
    coarse = np.stack(two(np.block([[cosine, sine], [-sine, cosine]])))

    cell = (8 * np.arange(quads)[:, None, None] + 2 * np.arange(pairs)[None, :, None] + sub_e[None, None, :])[..., None]
    angle = two_pi * cell * ids / NPIX
    sign = 1.0 - 2.0 * ((cell + ids) % 2)
    twist = np.stack([np.cos(angle) * sign, np.sin(angle) * sign], axis=2)
    e = 2 * np.arange(pairs)[None, :, None] + sub_e[None, None, :]
    angle = np.broadcast_to(two_pi * (np.arange(4)[:, None, None] * e)[..., None] / 32, (4, pairs, 8, LANES))
    inner = np.stack([np.cos(angle), np.sin(angle)], axis=2)
    twist = np.stack([twist, inner]).astype(f32)

    cell_size = 0.5 / NPIX
    screens = []
    for core in range(CORES):
        x = (strips[core][sub_l] - STRIP // 2) * cell_size
        column = ids[None, None, :] + LANES * (np.arange(16)[:, None, None] + 16 * sub_e[None, :, None])
        y = (column - NPIX // 2) * cell_size
        radius = x[None, :, None] ** 2 + y**2
        lowered = -radius / (1.0 + np.sqrt(1.0 - radius))
        w = w_step * (np.arange(planes) - 0.5 * (WPLANES - 1))
        angle = two_pi * w[:, None, None, None] * lowered[None]
        screens.append(np.stack([np.cos(angle), np.sin(angle)], axis=2))
    screen = np.stack(screens).astype(f32)
    return tap_table, coarse, twist, screen


def solve_taylor(moments, images):
    entry_00, entry_01, entry_02 = (moments[0], moments[1], moments[2])
    entry_11, entry_12, entry_22 = (moments[2], moments[3], moments[4])
    minor_00 = entry_11 * entry_22 - entry_12 * entry_12
    minor_01 = entry_02 * entry_12 - entry_01 * entry_22
    minor_02 = entry_01 * entry_12 - entry_02 * entry_11
    minor_11 = entry_00 * entry_22 - entry_02 * entry_02
    minor_12 = entry_01 * entry_02 - entry_00 * entry_12
    minor_22 = entry_00 * entry_11 - entry_01 * entry_01
    determinant = entry_00 * minor_00 + entry_01 * minor_01 + entry_02 * minor_02
    first = (minor_00 * images[0] + minor_01 * images[1] + minor_02 * images[2]) / determinant
    second = (minor_01 * images[0] + minor_11 * images[1] + minor_12 * images[2]) / determinant
    third = (minor_02 * images[0] + minor_12 * images[1] + minor_22 * images[2]) / determinant
    return first, second, third


def multiply(a, b):
    return a[0] * b[0] - a[1] * b[1], a[0] * b[1] + a[1] * b[0]


def radix4(x):
    a = (x[0][0] + x[2][0], x[0][1] + x[2][1])
    b = (x[0][0] - x[2][0], x[0][1] - x[2][1])
    c = (x[1][0] + x[3][0], x[1][1] + x[3][1])
    d = (x[1][0] - x[3][0], x[1][1] - x[3][1])
    return (
        (a[0] + c[0], a[1] + c[1]), (b[0] - d[1], b[1] + d[0]),
        (a[0] - c[0], a[1] - c[1]), (b[0] + d[1], b[1] - d[0]),
    )


def strip_kernel(
    n_chan, n_bl, count_ref, offset_ref, value_ref, weight_ref, kernel_ref, tile_ref, plane_ref, chan_ref,
    tap_hbm, coarse_hbm, twist_hbm, screen_hbm, out_ref,
    tap_ref, coarse_ref, twist_ref, screen_ref, meta_ref, meta_land, taps_land,
    high_ref, low_ref, dist_ref, grid_ref, mom_ref, spec_ref, acc_ref, img0_ref, img1_ref, img2_ref,
    xland_ref, sum_ref, bland_ref, msend_ref, mxland_ref, msum_ref, mbland_ref,
    load_sem, pair_send, pair_recv, x_send, x_recv, xm_send, xm_recv, b_send, b_recv, bm_send, bm_recv,
):
    chan = lax.axis_index("chan")
    bl = lax.axis_index("bl")
    core = lax.rem(chan, CORES)
    seat = chan // CORES
    n_seat = n_chan // CORES
    per = STRIP // n_chan
    img_refs = (img0_ref, img1_ref, img2_ref)
    slots = kernel_ref.shape[1]

    def seat_peer(d):
        return lax.rem(seat + d, n_seat)

    def bl_peer(d):
        return lax.rem(bl + d, n_bl)

    mate = (chan + 1 - 2 * core, bl)
    barrier = pltpu.get_barrier_semaphore()
    pl.semaphore_signal(barrier, inc=1, device_id=mate, device_id_type=MESH)
    for d in range(1, n_seat):
        pl.semaphore_signal(barrier, inc=1, device_id=(seat_peer(d) * CORES + core, bl), device_id_type=MESH)
    for d in range(1, n_bl):
        pl.semaphore_signal(barrier, inc=1, device_id=(chan, bl_peer(d)), device_id_type=MESH)

    loads = [
        pltpu.make_async_copy(source, target, load_sem.at[i])
        for i, (source, target) in enumerate((
            (tap_hbm.at[core], tap_ref), (coarse_hbm, coarse_ref),
            (twist_hbm, twist_ref), (screen_hbm.at[core], screen_ref),
        ))
    ]
    for load in loads:
        load.start()

    grid_ref[...] = jnp.zeros_like(grid_ref)
    mom_ref[...] = jnp.zeros_like(mom_ref)

    slot = lax.broadcasted_iota(jnp.int32, (1, slots), 1)
    tiles = tile_ref[...]
    plane = plane_ref[...]
    chans = chan_ref[...]
    coord = jnp.zeros((1, slots), jnp.float32)
    for c in range(offset_ref.shape[1]):
        coord = jnp.where(chans == c, offset_ref[0, c], coord)
    weight = jnp.where(slot < count_ref[0, 0], weight_ref[...].astype(jnp.float32), 0.0)
    value = value_ref[...].astype(jnp.float32)
    flip = plane >= planes
    v_tile = tiles & (ntiles - 1)
    v_tile = jnp.where(flip, ntiles - 1 - v_tile, v_tile)
    fold = jnp.where(flip, WPLANES - 1 - plane, plane)
    place = (fold * quads + (v_tile & (quads - 1))) * LANES + lax.shift_right_logical(v_tile, quads.bit_length() - 1)
    meta_ref[0:1, :] = weight * value[0:1]
    meta_ref[1:2, :] = weight * value[1:2]
    meta_ref[2:3, :] = coord
    meta_ref[3:4, :] = weight
    meta_ref[4:5, :] = (lax.shift_right_logical(tiles, ntiles.bit_length() - 1) - ntiles // 2).astype(jnp.float32)
    meta_ref[5:6, :] = place.astype(jnp.float32)
    meta_ref[6:7, :] = jnp.where(flip, -1.0, 1.0)
    meta_ref[7:8, :] = jnp.zeros((1, slots), jnp.float32)

    sub = lax.broadcasted_iota(jnp.int32, (8, 1), 0)
    first = sub < held
    local = lax.rem(sub, held)
    strip = (local // per * CORES + core) * per + lax.rem(local, per) - STRIP // 2
    turn = strip.astype(jnp.float32) * (1.0 / ntiles)
    quarter = jnp.where(first, 0.0, 0.25)

    loads[0].wait()

    def one_block(taps_ref, rows_ref, block, carry):
        here = pl.ds(pl.multiple_of(block * BLK, BLK), BLK)
        base_real = rows_ref[0:1, here]
        base_imag = rows_ref[1:2, here]
        coord = rows_ref[2:3, here]
        weight = rows_ref[3:4, here]
        u_off = rows_ref[4:5, here]
        place = rows_ref[5:6, here]
        sign = rows_ref[6:7, here]
        taps = taps_ref[:, here]
        plain = taps * jnp.maximum(sign, 0.0).astype(jnp.bfloat16)
        turned = taps * jnp.maximum(-sign, 0.0).astype(jnp.bfloat16)
        sums = jnp.dot(
            tap_ref[...], jnp.concatenate([plain, turned, plain, turned], axis=0),
            preferred_element_type=jnp.float32,
        )
        cycle = u_off * turn - quarter
        cycle = cycle - jnp.floor(cycle + 0.5)
        square = cycle * cycle
        wave = jnp.full_like(square, cos_terms[-1])
        for term in cos_terms[-2::-1]:
            wave = wave * square + term
        other = pltpu.roll(wave, held, 0)
        cosine = jnp.where(first, wave, other)
        sine = jnp.where(first, other, wave)
        z_real = base_real * cosine - base_imag * sine
        z_imag = base_real * sine + base_imag * cosine
        s_real = z_real * sign
        s_imag = z_imag * sign
        sum_real = sums[0:32].reshape(pairs, 8, BLK)
        sum_imag = sums[32:64].reshape(pairs, 8, BLK)
        part_real = (sum_real * z_real[None] - sum_imag * z_imag[None]).reshape(32, BLK)
        part_imag = (sum_real * s_imag[None] + sum_imag * s_real[None]).reshape(32, BLK)
        edge = sums[64:72] * jnp.where(first, z_real, s_imag) + sums[72:80] * jnp.where(first, -z_imag, s_real)
        part = jnp.concatenate([part_real, part_imag, edge], axis=0)
        parts = [part]
        for k in range(1, TAYLOR):
            parts.append(parts[-1] * coord)
        high, low = split(jnp.concatenate(parts, axis=0))
        high_ref[...] = high
        low_ref[...] = low

        weighted = weight * sums[80:81]
        power = weighted
        for m in range(MOMENTS):
            mom_ref[m : m + 1, :] += power
            power = power * coord

        lane = lax.broadcasted_iota(jnp.int32, (BLK, LANES), 1).astype(jnp.float32)
        column = jnp.transpose(jnp.broadcast_to(place, (LANES, BLK)))
        dist_ref[...] = column - lane
        for g in range(groups):
            hot = jnp.concatenate(
                [jnp.where(dist_ref[...] == float((2 * g + h) * LANES), 1.0, 0.0) for h in range(2)], axis=1
            ).astype(jnp.bfloat16)
            grid_ref[g] += jnp.dot(high_ref[...], hot, preferred_element_type=jnp.float32) + jnp.dot(
                low_ref[...], hot, preferred_element_type=jnp.float32
            )
        return carry

    blocks = slots // BLK
    lax.fori_loop(0, blocks // 2, functools.partial(one_block, kernel_ref, meta_ref), 0)
    pl.semaphore_wait(barrier, 1 + n_seat - 1 + n_bl - 1)
    swaps = [
        pltpu.make_async_remote_copy(
            src_ref=source, dst_ref=target, send_sem=pair_send.at[i], recv_sem=pair_recv.at[i],
            device_id=mate, device_id_type=MESH,
        )
        for i, (source, target) in enumerate(((kernel_ref, taps_land), (meta_ref, meta_land)))
    ]
    for swap in swaps:
        swap.start()
    lax.fori_loop(blocks // 2, blocks, functools.partial(one_block, kernel_ref, meta_ref), 0)
    for swap in swaps:
        swap.wait()
    lax.fori_loop(0, blocks, functools.partial(one_block, taps_land, meta_land), 0)

    msend_ref[...] = jnp.broadcast_to(jnp.sum(mom_ref[...], axis=1, keepdims=True), msend_ref.shape)
    mom_x = [
        pltpu.make_async_remote_copy(
            src_ref=msend_ref, dst_ref=mxland_ref.at[d], send_sem=xm_send.at[d], recv_sem=xm_recv.at[d],
            device_id=(seat_peer(d) * CORES + core, bl), device_id_type=MESH,
        )
        for d in range(1, n_seat)
    ]
    for copy in mom_x:
        copy.start()

    for load in loads[1:]:
        load.wait()
    flipper = jnp.where(first, 1.0, -1.0)
    spin = [
        (jnp.where(first, 1.0, float(np.cos(two_pi * s / 8))), jnp.where(first, 0.0, float(np.sin(two_pi * s / 8))))
        for s in range(4)
    ]

    def transform(k):
        low_row = k * per_k
        pieces = []
        for p in range(planes):
            edges = []
            for b in range(quads):
                q = p * quads + b
                lanes = pl.ds(q % 2 * LANES, LANES)
                edges.append(grid_ref[q // 2, low_row + 64 : low_row + 72, lanes])
            edges = [pltpu.roll(edges[-1], 1, 1)] + edges[:-1]
            for b in range(quads):
                q = p * quads + b
                lanes = pl.ds(q % 2 * LANES, LANES)
                real = grid_ref[q // 2, low_row : low_row + 32, lanes]
                imag = grid_ref[q // 2, low_row + 32 : low_row + 64, lanes]
                edge = edges[b]
                head_real = real[:8] + jnp.where(first, edge, 0.0)
                head_imag = imag[:8] + jnp.where(first, pltpu.roll(edge, held, 0), 0.0)
                real = jnp.concatenate([head_real, real[8:]], axis=0)
                imag = jnp.concatenate([head_imag, imag[8:]], axis=0)
                pieces.append(jnp.concatenate([real, imag], axis=1))
        high, low = split(jnp.concatenate(pieces, axis=0))
        spec_ref[...] = (
            jnp.dot(high, coarse_ref[0], preferred_element_type=jnp.float32)
            + jnp.dot(high, coarse_ref[1], preferred_element_type=jnp.float32)
            + jnp.dot(low, coarse_ref[0], preferred_element_type=jnp.float32)
        )
        acc_ref[...] = jnp.zeros_like(acc_ref)

        def one_plane(p, carry):
            inner = [[None] * pairs for r in range(4)]
            for t in range(pairs):
                column = []
                for b in range(quads):
                    row = pl.ds(pl.multiple_of((p * quads + b) * 32 + t * 8, 8), 8)
                    x = (spec_ref[row, :LANES], spec_ref[row, LANES:])
                    column.append(multiply(x, (twist_ref[0, b, t, 0], twist_ref[0, b, t, 1])))
                for r, z in enumerate(radix4(column)):
                    inner[r][t] = multiply(z, (twist_ref[1, r, t, 0], twist_ref[1, r, t, 1])) if r else z
            for r in range(4):
                for s, z in enumerate(radix4(inner[r])):
                    if s:
                        z = multiply(z, spin[s])
                    real = pltpu.roll(z[0], held, 0) + z[0] * flipper
                    imag = pltpu.roll(z[1], held, 0) + z[1] * flipper
                    at = r + 4 * s
                    acc_ref[at] += real * screen_ref[p, at, 0] - imag * screen_ref[p, at, 1]
            return carry

        lax.fori_loop(0, planes, one_plane, 0)
        for at in range(16):
            img_refs[k][pl.ds(at, 8, stride=16), :] = acc_ref[at]

    span = per * 16

    def x_copies(k):
        copies = []
        for d in range(1, n_seat):
            for h in range(2):
                row = pl.multiple_of((held * h + seat_peer(d) * per) * 16, 16)
                copies.append(
                    pltpu.make_async_remote_copy(
                        src_ref=img_refs[k].at[pl.ds(row, span), :], dst_ref=xland_ref.at[k, d, h],
                        send_sem=x_send.at[k, d, h], recv_sem=x_recv.at[k, d, h],
                        device_id=(seat_peer(d) * CORES + core, bl), device_id_type=MESH,
                    )
                )
        return copies

    def b_copies(k):
        return [
            pltpu.make_async_remote_copy(
                src_ref=sum_ref.at[k, bl_peer(d)], dst_ref=bland_ref.at[k, d],
                send_sem=b_send.at[k, d], recv_sem=b_recv.at[k, d],
                device_id=(chan, bl_peer(d)), device_id_type=MESH,
            )
            for d in range(1, n_bl)
        ]

    share = per * NPIX // (n_bl * LANES)

    def gather_x(k, copies):
        for copy in copies:
            copy.wait()
        for h in range(2):
            row = pl.multiple_of((held * h + seat * per) * 16, 16)
            total = img_refs[k][pl.ds(row, span), :]
            for d in range(1, n_seat):
                total = total + xland_ref[k, d, h]
            for i in range(per):
                at = (i * 32 + h * 16) // share
                sum_ref[k, at : at + 16 // share] = total[i * 16 : (i + 1) * 16].reshape(16 // share, share, LANES)
        copies = b_copies(k)
        for copy in copies:
            copy.start()
        return copies

    x_flight = []
    b_flight = []
    for k in range(TAYLOR):
        transform(k)
        x_flight.append(x_copies(k))
        for copy in x_flight[-1]:
            copy.start()
        if k == 0:
            for copy in mom_x:
                copy.wait()
            total = msend_ref[...]
            for d in range(1, n_seat):
                total = total + mxland_ref[d]
            msum_ref[...] = total
            mom_b = [
                pltpu.make_async_remote_copy(
                    src_ref=msum_ref, dst_ref=mbland_ref.at[d], send_sem=bm_send.at[d], recv_sem=bm_recv.at[d],
                    device_id=(chan, bl_peer(d)), device_id_type=MESH,
                )
                for d in range(1, n_bl)
            ]
            for copy in mom_b:
                copy.start()
        else:
            b_flight.append(gather_x(k - 1, x_flight[k - 1]))
    b_flight.append(gather_x(TAYLOR - 1, x_flight[-1]))

    moments = msum_ref[...]
    for d in range(1, n_bl):
        mom_b[d - 1].wait()
        moments = moments + mbland_ref[d]
    images = []
    for k in range(TAYLOR):
        total = sum_ref[k, bl]
        for d in range(1, n_bl):
            b_flight[k][d - 1].wait()
            total = total + bland_ref[k, d]
        images.append(total)
    solved = solve_taylor([moments[m : m + 1] for m in range(MOMENTS)], images)
    for k in range(TAYLOR):
        out_ref[k] = solved[k]


def strip_image(n_chan, n_bl, count, offsets, value, weight, kernel, tiles, plane, chans):
    consts = [jnp.asarray(t) for t in tables(n_chan)]
    tap_table, coarse, twist, screen = consts
    smem = pl.BlockSpec(memory_space=pltpu.SMEM)
    vmem = pl.BlockSpec(memory_space=pltpu.VMEM)
    hbm = pl.BlockSpec(memory_space=pl.ANY)
    slots = kernel.shape[1]
    n_seat = n_chan // CORES
    per = STRIP // n_chan
    share = per * NPIX // (n_bl * LANES)
    f32 = jnp.float32
    bf16 = jnp.bfloat16
    dma = pltpu.SemaphoreType.DMA
    scratch = [
        (tap_table.shape[1:], bf16), (coarse.shape, bf16), (twist.shape, f32), (screen.shape[1:], f32),
        ((8, slots), f32), ((8, slots), f32), (kernel.shape, bf16),
        ((rows_all, BLK), bf16), ((rows_all, BLK), bf16), ((BLK, LANES), f32),
        ((groups, rows_all, 2 * LANES), f32), ((8, BLK), f32), ((planes * quads * 32, 2 * LANES), f32),
        ((16, 8, LANES), f32), ((LANES, LANES), f32), ((LANES, LANES), f32), ((LANES, LANES), f32),
        ((TAYLOR, n_seat, 2, per * 16, LANES), f32),
        ((TAYLOR, n_bl, share, LANES), f32), ((TAYLOR, n_bl, share, LANES), f32),
        ((8, LANES), f32), ((n_seat, 8, LANES), f32), ((8, LANES), f32), ((n_bl, 8, LANES), f32),
    ]
    return pl.pallas_call(
        functools.partial(strip_kernel, n_chan, n_bl),
        out_shape=jax.ShapeDtypeStruct((TAYLOR, share, LANES), f32),
        in_specs=[smem, smem] + [vmem] * 6 + [hbm] * 4,
        out_specs=vmem,
        scratch_shapes=[pltpu.VMEM(shape, kind) for shape, kind in scratch]
        + [
            dma((4,)), dma((2,)), dma((2,)),
            dma((TAYLOR, n_seat, 2)), dma((TAYLOR, n_seat, 2)), dma((n_seat,)), dma((n_seat,)),
            dma((TAYLOR, n_bl)), dma((TAYLOR, n_bl)), dma((n_bl,)), dma((n_bl,)),
        ],
        compiler_params=pltpu.CompilerParams(
            vmem_limit_bytes=56 * 1024 * 1024, collective_id=0, has_side_effects=True
        ),
        name="strip_image",
    )(count, offsets, value, weight, kernel, tiles, plane, chans, *consts)


def solution(mesh):
    n_chan = mesh.shape["chan"]
    n_bl = mesh.shape["bl"]

    def body(vis_value, vis_weight, kernel, tile_index, plane_index, chan_index, chan_offset, counts):
        out = strip_image(
            n_chan, n_bl, counts, chan_offset, vis_value[0, 0], vis_weight[0], kernel[0, 0],
            tile_index[0], plane_index[0], chan_index[0],
        )
        return out.reshape(TAYLOR, -1)

    in_specs = (
        P("chan", "bl", None, None),
        P("chan", "bl", None),
        P("chan", "bl", None, None),
        P("chan", "bl", None),
        P("chan", "bl", None),
        P("chan", "bl", None),
        P("chan", None),
        P("chan", "bl"),
    )
    out_specs = P(None, ("chan", "bl"))
    return jax.shard_map(body, mesh=mesh, in_specs=in_specs, out_specs=out_specs, check_vma=False)
```

time: 51.7 us -> 32.2 us (0.62)
  Pallas kernels: 49.6 us -> 30.1 us
    pallas_call x2 -> x1, Pallas kernels: 49.6 us -> 30.1 us  [strip_image(): pl.pallas_call(functools.partial(strip_kernel, n_chan, n_bl), out_shape=j...]
where the time goes in v1:
time: 32.2 us; the launch traced here: 32 us
  Pallas kernels  30.1 us (93%)
  local copies, waits for them, and re-layouts  1.32 us (4%)
  between operations  0.66 us (2%)
    pallas_call x1, Pallas kernels, strip_image(): pl.pallas_call(functools.partial(strip_kernel, n_chan, n_bl), out_shape=j...  30.1 us
    unnamed x1, local copies, waits for them, and re-layouts  1.32 us

profile of v1, /device:TPU:0, one launch (start us, length us, event | category | flops | bytes accessed | tf_op | source)
XLA Modules:
  0.0 32.0 jit_solution(4296377978288855060)
XLA Ops:
  0.7 30.1 %strip_image.1 = f32[3,8,128]{2,1,0:T(8,128)} custom-call(s32[1,1]{1,0:T(1,128)S(6)} %copy.16.count_ref, f32[1,16]{1,0:T(1,128)} %offset_ref.1, bf16[2,2048]{1,0:T(2,128)(2,1)} %bitcast.12, bf16[1,2048]{1,0:T(2,128)(2,1)} %bitcast.13, bf16[64,2048]{1,0:T(8,128)(2,1)} %bitcast.10, s32[1,2048]{1,0:T(1,128)} %bitcast.14, s32[1,2048]{1,0:T(1,128)} %bitcast.15, ...), custom_call_target="tpu_custom_call" | custom-call | tf_op jit(solution)/shard_map/strip_image/pallas_call | solution.py:479
  30.7 1.3 %copy.15 = f32[1,3,8,128]{3,1,2,0:T(4,128)} copy(f32[1,3,8,128]{3,2,1,0:T(8,128)} %bitcast.11) | data formatting | bytes 24576

commit v2 on v1

--- a/solution.py
+++ b/solution.py
@@ -142,12 +142,14 @@
 
 
 def strip_kernel(
-    n_chan, n_bl, count_ref, offset_ref, value_ref, weight_ref, kernel_ref, tile_ref, plane_ref, chan_ref,
+    n_chan, n_bl, count_hbm, offset_hbm, value_hbm, weight_hbm, kernel_hbm, tile_hbm, plane_hbm, chan_hbm,
     tap_hbm, coarse_hbm, twist_hbm, screen_hbm, out_ref,
+    count_ref, offset_ref, value_ref, weight_ref, kernel_ref, tile_ref, plane_ref, chan_ref,
     tap_ref, coarse_ref, twist_ref, screen_ref, meta_ref, meta_land, taps_land,
-    high_ref, low_ref, dist_ref, grid_ref, mom_ref, spec_ref, acc_ref, img0_ref, img1_ref, img2_ref,
-    xland_ref, sum_ref, bland_ref, msend_ref, mxland_ref, msum_ref, mbland_ref,
-    load_sem, pair_send, pair_recv, x_send, x_recv, xm_send, xm_recv, b_send, b_recv, bm_send, bm_recv,
+    high0_ref, low0_ref, code0_ref, high1_ref, low1_ref, code1_ref,
+    grid_ref, mom_ref, spec_ref, acc_ref, img0_ref, img1_ref, img2_ref,
+    xland_ref, sum_ref, bland_ref, msend_ref, mland_ref,
+    load_sem, pair_send, pair_recv, x_send, x_recv, m_send, m_recv, b_send, b_recv,
 ):
     chan = lax.axis_index("chan")
     bl = lax.axis_index("bl")
@@ -165,25 +167,29 @@
         return lax.rem(bl + d, n_bl)
 
     mate = (chan + 1 - 2 * core, bl)
-    barrier = pltpu.get_barrier_semaphore()
-    pl.semaphore_signal(barrier, inc=1, device_id=mate, device_id_type=MESH)
-    for d in range(1, n_seat):
-        pl.semaphore_signal(barrier, inc=1, device_id=(seat_peer(d) * CORES + core, bl), device_id_type=MESH)
-    for d in range(1, n_bl):
-        pl.semaphore_signal(barrier, inc=1, device_id=(chan, bl_peer(d)), device_id_type=MESH)
-
     loads = [
         pltpu.make_async_copy(source, target, load_sem.at[i])
         for i, (source, target) in enumerate((
-            (tap_hbm.at[core], tap_ref), (coarse_hbm, coarse_ref),
+            (count_hbm, count_ref), (offset_hbm, offset_ref), (value_hbm, value_ref), (weight_hbm, weight_ref),
+            (tile_hbm, tile_ref), (plane_hbm, plane_ref), (chan_hbm, chan_ref),
+            (kernel_hbm, kernel_ref), (tap_hbm.at[core], tap_ref), (coarse_hbm, coarse_ref),
             (twist_hbm, twist_ref), (screen_hbm.at[core], screen_ref),
         ))
     ]
     for load in loads:
         load.start()
 
-    grid_ref[...] = jnp.zeros_like(grid_ref)
+    barrier = pltpu.get_barrier_semaphore()
+    pl.semaphore_signal(barrier, inc=1, device_id=mate, device_id_type=MESH)
+    peers = [(a, d) for a in range(n_seat) for d in range(n_bl) if a or d]
+    for a, d in peers:
+        pl.semaphore_signal(
+            barrier, inc=1, device_id=(seat_peer(a) * CORES + core, bl_peer(d)), device_id_type=MESH
+        )
+
     mom_ref[...] = jnp.zeros_like(mom_ref)
+    for load in loads[:7]:
+        load.wait()
 
     slot = lax.broadcasted_iota(jnp.int32, (1, slots), 1)
     tiles = tile_ref[...]
@@ -191,8 +197,8 @@
     chans = chan_ref[...]
     coord = jnp.zeros((1, slots), jnp.float32)
     for c in range(offset_ref.shape[1]):
-        coord = jnp.where(chans == c, offset_ref[0, c], coord)
-    weight = jnp.where(slot < count_ref[0, 0], weight_ref[...].astype(jnp.float32), 0.0)
+        coord = jnp.where(chans == c, offset_ref[0:1, c : c + 1], coord)
+    weight = jnp.where(slot < count_ref[...], weight_ref[...].astype(jnp.float32), 0.0)
     value = value_ref[...].astype(jnp.float32)
     flip = plane >= planes
     v_tile = tiles & (ntiles - 1)
@@ -215,10 +221,14 @@
     turn = strip.astype(jnp.float32) * (1.0 / ntiles)
     quarter = jnp.where(first, 0.0, 0.25)
 
-    loads[0].wait()
-
-    def one_block(taps_ref, rows_ref, block, carry):
-        here = pl.ds(pl.multiple_of(block * BLK, BLK), BLK)
+    for load in loads[7:9]:
+        load.wait()
+
+    buffers = ((high0_ref, low0_ref, code0_ref), (high1_ref, low1_ref, code1_ref))
+
+    def prepare(taps_ref, rows_ref, block, buffer):
+        high_ref, low_ref, code_ref = buffer
+        here = pl.ds(block * BLK, BLK)
         base_real = rows_ref[0:1, here]
         base_imag = rows_ref[1:2, here]
         coord = rows_ref[2:3, here]
@@ -267,19 +277,26 @@
 
         lane = lax.broadcasted_iota(jnp.int32, (BLK, LANES), 1).astype(jnp.float32)
         column = jnp.transpose(jnp.broadcast_to(place, (LANES, BLK)))
-        dist_ref[...] = column - lane
+        level = (column - lane) * (1.0 / LANES)
+        code_ref[...] = jnp.where(jnp.floor(level) == level, level, -1.0).astype(jnp.bfloat16)
+
+    def scatter(buffer, fresh):
+        high_ref, low_ref, code_ref = buffer
+        one = jnp.bfloat16(1.0)
+        zero = jnp.bfloat16(0.0)
         for g in range(groups):
             hot = jnp.concatenate(
-                [jnp.where(dist_ref[...] == float((2 * g + h) * LANES), 1.0, 0.0) for h in range(2)], axis=1
-            ).astype(jnp.bfloat16)
-            grid_ref[g] += jnp.dot(high_ref[...], hot, preferred_element_type=jnp.float32) + jnp.dot(
+                [jnp.where(code_ref[...] == jnp.bfloat16(2 * g + h), one, zero) for h in range(2)], axis=1
+            )
+            update = jnp.dot(high_ref[...], hot, preferred_element_type=jnp.float32) + jnp.dot(
                 low_ref[...], hot, preferred_element_type=jnp.float32
             )
-        return carry
+            if fresh:
+                grid_ref[g] = update
+            else:
+                grid_ref[g] += update
 
     blocks = slots // BLK
-    lax.fori_loop(0, blocks // 2, functools.partial(one_block, kernel_ref, meta_ref), 0)
-    pl.semaphore_wait(barrier, 1 + n_seat - 1 + n_bl - 1)
     swaps = [
         pltpu.make_async_remote_copy(
             src_ref=source, dst_ref=target, send_sem=pair_send.at[i], recv_sem=pair_recv.at[i],
@@ -287,25 +304,32 @@
         )
         for i, (source, target) in enumerate(((kernel_ref, taps_land), (meta_ref, meta_land)))
     ]
-    for swap in swaps:
-        swap.start()
-    lax.fori_loop(blocks // 2, blocks, functools.partial(one_block, kernel_ref, meta_ref), 0)
-    for swap in swaps:
-        swap.wait()
-    lax.fori_loop(0, blocks, functools.partial(one_block, taps_land, meta_land), 0)
+    order = [(kernel_ref, meta_ref, j) for j in range(blocks)] + [(taps_land, meta_land, j) for j in range(blocks)]
+    prepare(*order[0], buffers[0])
+    for j in range(2 * blocks):
+        if j == blocks // 2:
+            pl.semaphore_wait(barrier, 1 + n_seat * n_bl - 1)
+            for swap in swaps:
+                swap.start()
+        if j + 1 == blocks:
+            for swap in swaps:
+                swap.wait()
+        if j + 1 < 2 * blocks:
+            prepare(*order[j + 1], buffers[(j + 1) % 2])
+        scatter(buffers[j % 2], j == 0)
 
     msend_ref[...] = jnp.broadcast_to(jnp.sum(mom_ref[...], axis=1, keepdims=True), msend_ref.shape)
-    mom_x = [
+    mom_copies = [
         pltpu.make_async_remote_copy(
-            src_ref=msend_ref, dst_ref=mxland_ref.at[d], send_sem=xm_send.at[d], recv_sem=xm_recv.at[d],
-            device_id=(seat_peer(d) * CORES + core, bl), device_id_type=MESH,
+            src_ref=msend_ref, dst_ref=mland_ref.at[i], send_sem=m_send.at[i], recv_sem=m_recv.at[i],
+            device_id=(seat_peer(a) * CORES + core, bl_peer(d)), device_id_type=MESH,
         )
-        for d in range(1, n_seat)
+        for i, (a, d) in enumerate(peers)
     ]
-    for copy in mom_x:
+    for copy in mom_copies:
         copy.start()
 
-    for load in loads[1:]:
+    for load in loads[9:]:
         load.wait()
     flipper = jnp.where(first, 1.0, -1.0)
     spin = [
@@ -417,30 +441,13 @@
         x_flight.append(x_copies(k))
         for copy in x_flight[-1]:
             copy.start()
-        if k == 0:
-            for copy in mom_x:
-                copy.wait()
-            total = msend_ref[...]
-            for d in range(1, n_seat):
-                total = total + mxland_ref[d]
-            msum_ref[...] = total
-            mom_b = [
-                pltpu.make_async_remote_copy(
-                    src_ref=msum_ref, dst_ref=mbland_ref.at[d], send_sem=bm_send.at[d], recv_sem=bm_recv.at[d],
-                    device_id=(chan, bl_peer(d)), device_id_type=MESH,
-                )
-                for d in range(1, n_bl)
-            ]
-            for copy in mom_b:
-                copy.start()
-        else:
-            b_flight.append(gather_x(k - 1, x_flight[k - 1]))
-    b_flight.append(gather_x(TAYLOR - 1, x_flight[-1]))
-
-    moments = msum_ref[...]
-    for d in range(1, n_bl):
-        mom_b[d - 1].wait()
-        moments = moments + mbland_ref[d]
+    for k in range(TAYLOR):
+        b_flight.append(gather_x(k, x_flight[k]))
+
+    moments = msend_ref[...]
+    for i, copy in enumerate(mom_copies):
+        copy.wait()
+        moments = moments + mland_ref[i]
     images = []
     for k in range(TAYLOR):
         total = sum_ref[k, bl]
@@ -456,7 +463,6 @@
 def strip_image(n_chan, n_bl, count, offsets, value, weight, kernel, tiles, plane, chans):
     consts = [jnp.asarray(t) for t in tables(n_chan)]
     tap_table, coarse, twist, screen = consts
-    smem = pl.BlockSpec(memory_space=pltpu.SMEM)
     vmem = pl.BlockSpec(memory_space=pltpu.VMEM)
     hbm = pl.BlockSpec(memory_space=pl.ANY)
     slots = kernel.shape[1]
@@ -466,32 +472,35 @@
     f32 = jnp.float32
     bf16 = jnp.bfloat16
     dma = pltpu.SemaphoreType.DMA
-    scratch = [
+    block = [((rows_all, BLK), bf16), ((rows_all, BLK), bf16), ((BLK, LANES), bf16)]
+    inputs = (count, offsets, value, weight, kernel, tiles, plane, chans)
+    peers = n_seat * n_bl - 1
+    scratch = [(x.shape, x.dtype) for x in inputs] + [
         (tap_table.shape[1:], bf16), (coarse.shape, bf16), (twist.shape, f32), (screen.shape[1:], f32),
         ((8, slots), f32), ((8, slots), f32), (kernel.shape, bf16),
-        ((rows_all, BLK), bf16), ((rows_all, BLK), bf16), ((BLK, LANES), f32),
+        *block, *block,
         ((groups, rows_all, 2 * LANES), f32), ((8, BLK), f32), ((planes * quads * 32, 2 * LANES), f32),
         ((16, 8, LANES), f32), ((LANES, LANES), f32), ((LANES, LANES), f32), ((LANES, LANES), f32),
         ((TAYLOR, n_seat, 2, per * 16, LANES), f32),
         ((TAYLOR, n_bl, share, LANES), f32), ((TAYLOR, n_bl, share, LANES), f32),
-        ((8, LANES), f32), ((n_seat, 8, LANES), f32), ((8, LANES), f32), ((n_bl, 8, LANES), f32),
+        ((8, LANES), f32), ((peers, 8, LANES), f32),
     ]
     return pl.pallas_call(
         functools.partial(strip_kernel, n_chan, n_bl),
         out_shape=jax.ShapeDtypeStruct((TAYLOR, share, LANES), f32),
-        in_specs=[smem, smem] + [vmem] * 6 + [hbm] * 4,
+        in_specs=[hbm] * (len(inputs) + len(consts)),
         out_specs=vmem,
         scratch_shapes=[pltpu.VMEM(shape, kind) for shape, kind in scratch]
         + [
-            dma((4,)), dma((2,)), dma((2,)),
-            dma((TAYLOR, n_seat, 2)), dma((TAYLOR, n_seat, 2)), dma((n_seat,)), dma((n_seat,)),
-            dma((TAYLOR, n_bl)), dma((TAYLOR, n_bl)), dma((n_bl,)), dma((n_bl,)),
+            dma((len(inputs) + len(consts),)), dma((2,)), dma((2,)),
+            dma((TAYLOR, n_seat, 2)), dma((TAYLOR, n_seat, 2)), dma((peers,)), dma((peers,)),
+            dma((TAYLOR, n_bl)), dma((TAYLOR, n_bl)),
         ],
         compiler_params=pltpu.CompilerParams(
             vmem_limit_bytes=56 * 1024 * 1024, collective_id=0, has_side_effects=True
         ),
         name="strip_image",
-    )(count, offsets, value, weight, kernel, tiles, plane, chans, *consts)
+    )(*inputs, *consts)
 
 
 def solution(mesh):

time: 32.2 us -> 27.7 us (0.86)
  Pallas kernels: 30.1 us -> 25.5 us
    pallas_call x1, Pallas kernels: 30.1 us -> 25.5 us  [strip_image(): pl.pallas_call(functools.partial(strip_kernel, n_chan, n_bl), out_shape=j...]
where the time goes in v2:
time: 27.7 us; the launch traced here: 27.5 us
  Pallas kernels  25.5 us (92%)
  local copies, waits for them, and re-layouts  1.32 us (5%)
  between operations  0.66 us (2%)
    pallas_call x1, Pallas kernels, strip_image(): pl.pallas_call(functools.partial(strip_kernel, n_chan, n_bl), out_shape=j...  25.5 us
    unnamed x1, local copies, waits for them, and re-layouts  1.32 us

profile of v2, /device:TPU:0, one launch (start us, length us, event | category | flops | bytes accessed | tf_op | source)
XLA Modules:
  0.0 27.5 jit_solution(10211288705117611653)
XLA Ops:
  0.7 25.5 %strip_image.1 = f32[3,8,128]{2,1,0:T(8,128)} custom-call(s32[1,1]{1,0:T(1,128)S(6)} %copy.16.count_hbm, f32[1,16]{1,0:T(1,128)} %offset_hbm.1, bf16[2,2048]{1,0:T(2,128)(2,1)} %bitcast.12, bf16[1,2048]{1,0:T(2,128)(2,1)} %bitcast.13, bf16[64,2048]{1,0:T(8,128)(2,1)} %bitcast.10, s32[1,2048]{1,0:T(1,128)} %bitcast.14, s32[1,2048]{1,0:T(1,128)} %bitcast.15, ...), custom_call_target="tpu_custom_call" | custom-call | tf_op jit(solution)/shard_map/strip_image/pallas_call | solution.py:488
  26.2 1.3 %copy.15 = f32[1,3,8,128]{3,1,2,0:T(4,128)} copy(f32[1,3,8,128]{3,2,1,0:T(8,128)} %bitcast.11) | data formatting | bytes 24576

commit v3 on v2

--- a/solution.py
+++ b/solution.py
@@ -307,7 +307,7 @@
     order = [(kernel_ref, meta_ref, j) for j in range(blocks)] + [(taps_land, meta_land, j) for j in range(blocks)]
     prepare(*order[0], buffers[0])
     for j in range(2 * blocks):
-        if j == blocks // 2:
+        if j == 1:
             pl.semaphore_wait(barrier, 1 + n_seat * n_bl - 1)
             for swap in swaps:
                 swap.start()
@@ -359,20 +359,19 @@
                 imag = jnp.concatenate([head_imag, imag[8:]], axis=0)
                 pieces.append(jnp.concatenate([real, imag], axis=1))
         high, low = split(jnp.concatenate(pieces, axis=0))
-        spec_ref[...] = (
+        spec_ref[k] = (
             jnp.dot(high, coarse_ref[0], preferred_element_type=jnp.float32)
             + jnp.dot(high, coarse_ref[1], preferred_element_type=jnp.float32)
             + jnp.dot(low, coarse_ref[0], preferred_element_type=jnp.float32)
         )
-        acc_ref[...] = jnp.zeros_like(acc_ref)
-
-        def one_plane(p, carry):
+
+        def one_plane(p):
             inner = [[None] * pairs for r in range(4)]
             for t in range(pairs):
                 column = []
                 for b in range(quads):
-                    row = pl.ds(pl.multiple_of((p * quads + b) * 32 + t * 8, 8), 8)
-                    x = (spec_ref[row, :LANES], spec_ref[row, LANES:])
+                    row = pl.ds((p * quads + b) * 32 + t * 8, 8)
+                    x = (spec_ref[k, row, :LANES], spec_ref[k, row, LANES:])
                     column.append(multiply(x, (twist_ref[0, b, t, 0], twist_ref[0, b, t, 1])))
                 for r, z in enumerate(radix4(column)):
                     inner[r][t] = multiply(z, (twist_ref[1, r, t, 0], twist_ref[1, r, t, 1])) if r else z
@@ -383,12 +382,13 @@
                     real = pltpu.roll(z[0], held, 0) + z[0] * flipper
                     imag = pltpu.roll(z[1], held, 0) + z[1] * flipper
                     at = r + 4 * s
-                    acc_ref[at] += real * screen_ref[p, at, 0] - imag * screen_ref[p, at, 1]
-            return carry
-
-        lax.fori_loop(0, planes, one_plane, 0)
+                    term = real * screen_ref[p, at, 0] - imag * screen_ref[p, at, 1]
+                    acc_ref[k, at] = acc_ref[k, at] + term if p else term
+
+        for p in range(planes):
+            one_plane(p)
         for at in range(16):
-            img_refs[k][pl.ds(at, 8, stride=16), :] = acc_ref[at]
+            img_refs[k][pl.ds(at, 8, stride=16), :] = acc_ref[k, at]
 
     span = per * 16
 
@@ -479,15 +479,15 @@
         (tap_table.shape[1:], bf16), (coarse.shape, bf16), (twist.shape, f32), (screen.shape[1:], f32),
         ((8, slots), f32), ((8, slots), f32), (kernel.shape, bf16),
         *block, *block,
-        ((groups, rows_all, 2 * LANES), f32), ((8, BLK), f32), ((planes * quads * 32, 2 * LANES), f32),
-        ((16, 8, LANES), f32), ((LANES, LANES), f32), ((LANES, LANES), f32), ((LANES, LANES), f32),
+        ((groups, rows_all, 2 * LANES), f32), ((8, BLK), f32), ((TAYLOR, planes * quads * 32, 2 * LANES), f32),
+        ((TAYLOR, 16, 8, LANES), f32), ((LANES, LANES), f32), ((LANES, LANES), f32), ((LANES, LANES), f32),
         ((TAYLOR, n_seat, 2, per * 16, LANES), f32),
         ((TAYLOR, n_bl, share, LANES), f32), ((TAYLOR, n_bl, share, LANES), f32),
         ((8, LANES), f32), ((peers, 8, LANES), f32),
     ]
     return pl.pallas_call(
         functools.partial(strip_kernel, n_chan, n_bl),
-        out_shape=jax.ShapeDtypeStruct((TAYLOR, share, LANES), f32),
+        out_shape=pltpu.VMEM((TAYLOR, share, LANES), f32),
         in_specs=[hbm] * (len(inputs) + len(consts)),
         out_specs=vmem,
         scratch_shapes=[pltpu.VMEM(shape, kind) for shape, kind in scratch]

time: 27.7 us -> 25.4 us (0.917)
  Pallas kernels: 25.5 us -> 23.9 us
  local copies, waits for them, and re-layouts: 1.32 us -> 0.61 us
    pallas_call x1, Pallas kernels: 25.5 us -> 23.9 us  [strip_image(): pl.pallas_call(functools.partial(strip_kernel, n_chan, n_bl), out_shape=p...]
    unnamed x1, local copies, waits for them, and re-layouts: 1.32 us -> 0.61 us
where the time goes in v3:
time: 25.4 us; the launch traced here: 25.2 us
  Pallas kernels  23.9 us (94%)
  between operations  0.66 us (3%)
  local copies, waits for them, and re-layouts  0.61 us (2%)
    pallas_call x1, Pallas kernels, strip_image(): pl.pallas_call(functools.partial(strip_kernel, n_chan, n_bl), out_shape=p...  23.9 us
    unnamed x1, local copies, waits for them, and re-layouts  0.61 us

profile of v3, /device:TPU:0, one launch (start us, length us, event | category | flops | bytes accessed | tf_op | source)
XLA Modules:
  0.0 25.2 jit_solution(16663962090947482260)
XLA Ops:
  0.7 23.9 %strip_image.1 = f32[3,8,128]{2,1,0:T(8,128)S(1)} custom-call(s32[1,1]{1,0:T(1,128)S(6)} %copy.16.count_hbm, f32[1,16]{1,0:T(1,128)} %offset_hbm.1, bf16[2,2048]{1,0:T(2,128)(2,1)} %bitcast.12, bf16[1,2048]{1,0:T(2,128)(2,1)} %bitcast.13, bf16[64,2048]{1,0:T(8,128)(2,1)} %bitcast.11, s32[1,2048]{1,0:T(1,128)} %bitcast.14, s32[1,2048]{1,0:T(1,128)} %bitcast.15, ...), custom_call_target="tpu_custom_call" | custom-call | tf_op jit(solution)/shard_map/strip_image/pallas_call | solution.py:488
  24.6 0.6 %copy.15 = f32[1,3,8,128]{3,1,2,0:T(4,128)} copy(f32[1,3,8,128]{3,2,1,0:T(8,128)S(1)} %bitcast.10) | data formatting | bytes 24576

commit v4 on v3

--- a/solution.py
+++ b/solution.py
@@ -28,6 +28,8 @@
 per_k = TILE * STRIP + 8
 rows_all = TAYLOR * per_k
 BLK = 512
+low_scale = 256.0
+f8 = jnp.float8_e4m3fn
 MESH = pl.DeviceIdType.MESH
 
 
@@ -148,8 +150,8 @@
     tap_ref, coarse_ref, twist_ref, screen_ref, meta_ref, meta_land, taps_land,
     high0_ref, low0_ref, code0_ref, high1_ref, low1_ref, code1_ref,
     grid_ref, mom_ref, spec_ref, acc_ref, img0_ref, img1_ref, img2_ref,
-    xland_ref, sum_ref, bland_ref, msend_ref, mland_ref,
-    load_sem, pair_send, pair_recv, x_send, x_recv, m_send, m_recv, b_send, b_recv,
+    xland_ref, sum_ref, bland_ref, msend_ref, mxland_ref, msum_ref, mland_ref,
+    load_sem, pair_send, pair_recv, x_send, x_recv, xm_send, xm_recv, b_send, b_recv, bm_send, bm_recv,
 ):
     chan = lax.axis_index("chan")
     bl = lax.axis_index("bl")
@@ -181,11 +183,10 @@
 
     barrier = pltpu.get_barrier_semaphore()
     pl.semaphore_signal(barrier, inc=1, device_id=mate, device_id_type=MESH)
-    peers = [(a, d) for a in range(n_seat) for d in range(n_bl) if a or d]
-    for a, d in peers:
-        pl.semaphore_signal(
-            barrier, inc=1, device_id=(seat_peer(a) * CORES + core, bl_peer(d)), device_id_type=MESH
-        )
+    for d in range(1, n_seat):
+        pl.semaphore_signal(barrier, inc=1, device_id=(seat_peer(d) * CORES + core, bl), device_id_type=MESH)
+    for d in range(1, n_bl):
+        pl.semaphore_signal(barrier, inc=1, device_id=(chan, bl_peer(d)), device_id_type=MESH)
 
     mom_ref[...] = jnp.zeros_like(mom_ref)
     for load in loads[:7]:
@@ -265,9 +266,10 @@
         parts = [part]
         for k in range(1, TAYLOR):
             parts.append(parts[-1] * coord)
-        high, low = split(jnp.concatenate(parts, axis=0))
+        parts = jnp.concatenate(parts, axis=0)
+        high = parts.astype(jnp.bfloat16)
         high_ref[...] = high
-        low_ref[...] = low
+        low_ref[...] = ((parts - high.astype(jnp.float32)) * low_scale).astype(f8)
 
         weighted = weight * sums[80:81]
         power = weighted
@@ -278,19 +280,18 @@
         lane = lax.broadcasted_iota(jnp.int32, (BLK, LANES), 1).astype(jnp.float32)
         column = jnp.transpose(jnp.broadcast_to(place, (LANES, BLK)))
         level = (column - lane) * (1.0 / LANES)
-        code_ref[...] = jnp.where(jnp.floor(level) == level, level, -1.0).astype(jnp.bfloat16)
+        code = jnp.where(jnp.floor(level) == level, level, -1.0).astype(jnp.bfloat16)
+        one = jnp.bfloat16(1.0)
+        zero = jnp.bfloat16(0.0)
+        for q in range(planes * quads):
+            code_ref[:, q * LANES : (q + 1) * LANES] = jnp.where(code == jnp.bfloat16(q), one, zero).astype(f8)
 
     def scatter(buffer, fresh):
         high_ref, low_ref, code_ref = buffer
-        one = jnp.bfloat16(1.0)
-        zero = jnp.bfloat16(0.0)
         for g in range(groups):
-            hot = jnp.concatenate(
-                [jnp.where(code_ref[...] == jnp.bfloat16(2 * g + h), one, zero) for h in range(2)], axis=1
-            )
-            update = jnp.dot(high_ref[...], hot, preferred_element_type=jnp.float32) + jnp.dot(
-                low_ref[...], hot, preferred_element_type=jnp.float32
-            )
+            hot = code_ref[:, g * 2 * LANES : (g + 1) * 2 * LANES]
+            rest = jnp.dot(low_ref[...], hot, preferred_element_type=jnp.float32)
+            update = jnp.dot(high_ref[...], hot, preferred_element_type=jnp.float32) + rest * (1.0 / low_scale)
             if fresh:
                 grid_ref[g] = update
             else:
@@ -308,7 +309,7 @@
     prepare(*order[0], buffers[0])
     for j in range(2 * blocks):
         if j == 1:
-            pl.semaphore_wait(barrier, 1 + n_seat * n_bl - 1)
+            pl.semaphore_wait(barrier, 1 + n_seat - 1 + n_bl - 1)
             for swap in swaps:
                 swap.start()
         if j + 1 == blocks:
@@ -319,15 +320,15 @@
         scatter(buffers[j % 2], j == 0)
 
     msend_ref[...] = jnp.broadcast_to(jnp.sum(mom_ref[...], axis=1, keepdims=True), msend_ref.shape)
-    mom_copies = [
+    def drain(ref, send, recv):
+        pltpu.make_async_copy(ref, ref, send).wait()
+        pltpu.make_async_copy(ref, ref, recv).wait()
+
+    for d in range(1, n_seat):
         pltpu.make_async_remote_copy(
-            src_ref=msend_ref, dst_ref=mland_ref.at[i], send_sem=m_send.at[i], recv_sem=m_recv.at[i],
-            device_id=(seat_peer(a) * CORES + core, bl_peer(d)), device_id_type=MESH,
-        )
-        for i, (a, d) in enumerate(peers)
-    ]
-    for copy in mom_copies:
-        copy.start()
+            src_ref=msend_ref, dst_ref=mxland_ref.at[d - 1], send_sem=xm_send, recv_sem=xm_recv,
+            device_id=(seat_peer(d) * CORES + core, bl), device_id_type=MESH,
+        ).start()
 
     for load in loads[9:]:
         load.wait()
@@ -392,68 +393,64 @@
 
     span = per * 16
 
-    def x_copies(k):
-        copies = []
+    def send_x(k):
         for d in range(1, n_seat):
             for h in range(2):
                 row = pl.multiple_of((held * h + seat_peer(d) * per) * 16, 16)
-                copies.append(
-                    pltpu.make_async_remote_copy(
-                        src_ref=img_refs[k].at[pl.ds(row, span), :], dst_ref=xland_ref.at[k, d, h],
-                        send_sem=x_send.at[k, d, h], recv_sem=x_recv.at[k, d, h],
-                        device_id=(seat_peer(d) * CORES + core, bl), device_id_type=MESH,
-                    )
-                )
-        return copies
-
-    def b_copies(k):
-        return [
+                pltpu.make_async_remote_copy(
+                    src_ref=img_refs[k].at[pl.ds(row, span), :], dst_ref=xland_ref.at[k, d - 1, h],
+                    send_sem=x_send.at[k], recv_sem=x_recv.at[k],
+                    device_id=(seat_peer(d) * CORES + core, bl), device_id_type=MESH,
+                ).start()
+
+    def send_b(k):
+        for d in range(1, n_bl):
             pltpu.make_async_remote_copy(
-                src_ref=sum_ref.at[k, bl_peer(d)], dst_ref=bland_ref.at[k, d],
-                send_sem=b_send.at[k, d], recv_sem=b_recv.at[k, d],
+                src_ref=sum_ref.at[k, bl_peer(d)], dst_ref=bland_ref.at[k, d - 1],
+                send_sem=b_send.at[k], recv_sem=b_recv.at[k],
                 device_id=(chan, bl_peer(d)), device_id_type=MESH,
-            )
-            for d in range(1, n_bl)
-        ]
+            ).start()
 
     share = per * NPIX // (n_bl * LANES)
 
-    def gather_x(k, copies):
-        for copy in copies:
-            copy.wait()
+    def gather_x(k):
+        drain(xland_ref.at[k], x_send.at[k], x_recv.at[k])
         for h in range(2):
             row = pl.multiple_of((held * h + seat * per) * 16, 16)
             total = img_refs[k][pl.ds(row, span), :]
             for d in range(1, n_seat):
-                total = total + xland_ref[k, d, h]
+                total = total + xland_ref[k, d - 1, h]
             for i in range(per):
                 at = (i * 32 + h * 16) // share
                 sum_ref[k, at : at + 16 // share] = total[i * 16 : (i + 1) * 16].reshape(16 // share, share, LANES)
-        copies = b_copies(k)
-        for copy in copies:
-            copy.start()
-        return copies
-
-    x_flight = []
-    b_flight = []
+        send_b(k)
+
     for k in range(TAYLOR):
         transform(k)
-        x_flight.append(x_copies(k))
-        for copy in x_flight[-1]:
-            copy.start()
+        send_x(k)
+    drain(mxland_ref, xm_send, xm_recv)
+    total = msend_ref[...]
+    for d in range(1, n_seat):
+        total = total + mxland_ref[d - 1]
+    msum_ref[...] = total
+    for d in range(1, n_bl):
+        pltpu.make_async_remote_copy(
+            src_ref=msum_ref, dst_ref=mland_ref.at[d - 1], send_sem=bm_send, recv_sem=bm_recv,
+            device_id=(chan, bl_peer(d)), device_id_type=MESH,
+        ).start()
     for k in range(TAYLOR):
-        b_flight.append(gather_x(k, x_flight[k]))
-
-    moments = msend_ref[...]
-    for i, copy in enumerate(mom_copies):
-        copy.wait()
-        moments = moments + mland_ref[i]
+        gather_x(k)
+
+    drain(mland_ref, bm_send, bm_recv)
+    moments = msum_ref[...]
+    for d in range(1, n_bl):
+        moments = moments + mland_ref[d - 1]
     images = []
     for k in range(TAYLOR):
+        drain(bland_ref.at[k], b_send.at[k], b_recv.at[k])
         total = sum_ref[k, bl]
         for d in range(1, n_bl):
-            b_flight[k][d - 1].wait()
-            total = total + bland_ref[k, d]
+            total = total + bland_ref[k, d - 1]
         images.append(total)
     solved = solve_taylor([moments[m : m + 1] for m in range(MOMENTS)], images)
     for k in range(TAYLOR):
@@ -472,18 +469,17 @@
     f32 = jnp.float32
     bf16 = jnp.bfloat16
     dma = pltpu.SemaphoreType.DMA
-    block = [((rows_all, BLK), bf16), ((rows_all, BLK), bf16), ((BLK, LANES), bf16)]
+    block = [((rows_all, BLK), bf16), ((rows_all, BLK), f8), ((BLK, planes * ntiles), f8)]
     inputs = (count, offsets, value, weight, kernel, tiles, plane, chans)
-    peers = n_seat * n_bl - 1
     scratch = [(x.shape, x.dtype) for x in inputs] + [
         (tap_table.shape[1:], bf16), (coarse.shape, bf16), (twist.shape, f32), (screen.shape[1:], f32),
         ((8, slots), f32), ((8, slots), f32), (kernel.shape, bf16),
         *block, *block,
         ((groups, rows_all, 2 * LANES), f32), ((8, BLK), f32), ((TAYLOR, planes * quads * 32, 2 * LANES), f32),
         ((TAYLOR, 16, 8, LANES), f32), ((LANES, LANES), f32), ((LANES, LANES), f32), ((LANES, LANES), f32),
-        ((TAYLOR, n_seat, 2, per * 16, LANES), f32),
-        ((TAYLOR, n_bl, share, LANES), f32), ((TAYLOR, n_bl, share, LANES), f32),
-        ((8, LANES), f32), ((peers, 8, LANES), f32),
+        ((TAYLOR, n_seat - 1, 2, per * 16, LANES), f32),
+        ((TAYLOR, n_bl, share, LANES), f32), ((TAYLOR, n_bl - 1, share, LANES), f32),
+        ((8, LANES), f32), ((n_seat - 1, 8, LANES), f32), ((8, LANES), f32), ((n_bl - 1, 8, LANES), f32),
     ]
     return pl.pallas_call(
         functools.partial(strip_kernel, n_chan, n_bl),
@@ -493,8 +489,7 @@
         scratch_shapes=[pltpu.VMEM(shape, kind) for shape, kind in scratch]
         + [
             dma((len(inputs) + len(consts),)), dma((2,)), dma((2,)),
-            dma((TAYLOR, n_seat, 2)), dma((TAYLOR, n_seat, 2)), dma((peers,)), dma((peers,)),
-            dma((TAYLOR, n_bl)), dma((TAYLOR, n_bl)),
+            dma((TAYLOR,)), dma((TAYLOR,)), dma, dma, dma((TAYLOR,)), dma((TAYLOR,)), dma, dma,
         ],
         compiler_params=pltpu.CompilerParams(
             vmem_limit_bytes=56 * 1024 * 1024, collective_id=0, has_side_effects=True

time: 25.4 us -> 23.8 us (0.937)
  Pallas kernels: 23.9 us -> 22.4 us
    pallas_call x1, Pallas kernels: 23.9 us -> 22.4 us  [strip_image(): pl.pallas_call(functools.partial(strip_kernel, n_chan, n_bl), out_shape=p...]
where the time goes in v4:
time: 23.8 us; the launch traced here: 23.7 us
  Pallas kernels  22.4 us (94%)
  between operations  0.66 us (3%)
  local copies, waits for them, and re-layouts  0.61 us (3%)
    pallas_call x1, Pallas kernels, strip_image(): pl.pallas_call(functools.partial(strip_kernel, n_chan, n_bl), out_shape=p...  22.4 us
    unnamed x1, local copies, waits for them, and re-layouts  0.61 us

profile of v4, /device:TPU:0, one launch (start us, length us, event | category | flops | bytes accessed | tf_op | source)
XLA Modules:
  0.0 23.7 jit_solution(842924280737221284)
XLA Ops:
  0.7 22.4 %strip_image.1 = f32[3,8,128]{2,1,0:T(8,128)S(1)} custom-call(s32[1,1]{1,0:T(1,128)S(6)} %copy.16.count_hbm, f32[1,16]{1,0:T(1,128)} %offset_hbm.1, bf16[2,2048]{1,0:T(2,128)(2,1)} %bitcast.12, bf16[1,2048]{1,0:T(2,128)(2,1)} %bitcast.13, bf16[64,2048]{1,0:T(8,128)(2,1)} %bitcast.11, s32[1,2048]{1,0:T(1,128)} %bitcast.14, s32[1,2048]{1,0:T(1,128)} %bitcast.15, ...), custom_call_target="tpu_custom_call" | custom-call | tf_op jit(solution)/shard_map/strip_image/pallas_call | solution.py:484
  23.0 0.6 %copy.15 = f32[1,3,8,128]{3,1,2,0:T(4,128)} copy(f32[1,3,8,128]{3,2,1,0:T(8,128)S(1)} %bitcast.10) | data formatting | bytes 24576

commit v5 on v4

--- a/solution.py
+++ b/solution.py
@@ -85,17 +85,18 @@
 
     ids = np.arange(LANES)
     angle = two_pi * (ids[:, None] * ids[None, :] % LANES) / LANES
-    cosine, sine = np.cos(angle), np.sin(angle)
-    coarse = np.stack(two(np.block([[cosine, sine], [-sine, cosine]])))
-
-    cell = (8 * np.arange(quads)[:, None, None] + 2 * np.arange(pairs)[None, :, None] + sub_e[None, None, :])[..., None]
-    angle = two_pi * cell * ids / NPIX
-    sign = 1.0 - 2.0 * ((cell + ids) % 2)
-    twist = np.stack([np.cos(angle) * sign, np.sin(angle) * sign], axis=2)
-    e = 2 * np.arange(pairs)[None, :, None] + sub_e[None, None, :]
-    angle = np.broadcast_to(two_pi * (np.arange(4)[:, None, None] * e)[..., None] / 32, (4, pairs, 8, LANES))
-    inner = np.stack([np.cos(angle), np.sin(angle)], axis=2)
-    twist = np.stack([twist, inner]).astype(f32)
+    coarse = []
+    for b in range(quads):
+        angle = two_pi * (ids[:, None] * ids[None, :] % LANES) / LANES + two_pi * 8 * b * ids[None, :] / NPIX
+        cosine, sine = np.cos(angle), np.sin(angle)
+        coarse.append(np.stack(two(np.block([[cosine, sine], [-sine, cosine]]))))
+    coarse = np.stack(coarse)
+
+    e = (2 * np.arange(pairs)[:, None] + sub_e[None, :])[..., None]
+    column = ids + LANES * np.arange(4)[:, None, None, None]
+    sign = 1.0 - 2.0 * ((e + column) % 2)
+    angle = two_pi * e * column / NPIX
+    twist = np.stack([np.cos(angle) * sign, np.sin(angle) * sign], axis=2).astype(f32)
 
     cell_size = 0.5 / NPIX
     screens = []
@@ -149,7 +150,7 @@
     count_ref, offset_ref, value_ref, weight_ref, kernel_ref, tile_ref, plane_ref, chan_ref,
     tap_ref, coarse_ref, twist_ref, screen_ref, meta_ref, meta_land, taps_land,
     high0_ref, low0_ref, code0_ref, high1_ref, low1_ref, code1_ref,
-    grid_ref, mom_ref, spec_ref, acc_ref, img0_ref, img1_ref, img2_ref,
+    grid0_ref, grid1_ref, grid2_ref, mom_ref, spec_ref, acc_ref, img0_ref, img1_ref, img2_ref,
     xland_ref, sum_ref, bland_ref, msend_ref, mxland_ref, msum_ref, mland_ref,
     load_sem, pair_send, pair_recv, x_send, x_recv, xm_send, xm_recv, b_send, b_recv, bm_send, bm_recv,
 ):
@@ -178,7 +179,7 @@
             (twist_hbm, twist_ref), (screen_hbm.at[core], screen_ref),
         ))
     ]
-    for load in loads:
+    for load in loads[7:9] + loads[:7] + loads[9:]:
         load.start()
 
     barrier = pltpu.get_barrier_semaphore()
@@ -229,7 +230,8 @@
 
     def prepare(taps_ref, rows_ref, block, buffer):
         high_ref, low_ref, code_ref = buffer
-        here = pl.ds(block * BLK, BLK)
+        start, size = block
+        here = pl.ds(start, size)
         base_real = rows_ref[0:1, here]
         base_imag = rows_ref[1:2, here]
         coord = rows_ref[2:3, here]
@@ -257,10 +259,10 @@
         z_imag = base_real * sine + base_imag * cosine
         s_real = z_real * sign
         s_imag = z_imag * sign
-        sum_real = sums[0:32].reshape(pairs, 8, BLK)
-        sum_imag = sums[32:64].reshape(pairs, 8, BLK)
-        part_real = (sum_real * z_real[None] - sum_imag * z_imag[None]).reshape(32, BLK)
-        part_imag = (sum_real * s_imag[None] + sum_imag * s_real[None]).reshape(32, BLK)
+        sum_real = sums[0:32].reshape(pairs, 8, size)
+        sum_imag = sums[32:64].reshape(pairs, 8, size)
+        part_real = (sum_real * z_real[None] - sum_imag * z_imag[None]).reshape(32, size)
+        part_imag = (sum_real * s_imag[None] + sum_imag * s_real[None]).reshape(32, size)
         edge = sums[64:72] * jnp.where(first, z_real, s_imag) + sums[72:80] * jnp.where(first, -z_imag, s_real)
         part = jnp.concatenate([part_real, part_imag, edge], axis=0)
         parts = [part]
@@ -268,36 +270,40 @@
             parts.append(parts[-1] * coord)
         parts = jnp.concatenate(parts, axis=0)
         high = parts.astype(jnp.bfloat16)
-        high_ref[...] = high
-        low_ref[...] = ((parts - high.astype(jnp.float32)) * low_scale).astype(f8)
+        high_ref[:, :size] = high
+        low_ref[:, :size] = ((parts - high.astype(jnp.float32)) * low_scale).astype(f8)
 
         weighted = weight * sums[80:81]
         power = weighted
         for m in range(MOMENTS):
-            mom_ref[m : m + 1, :] += power
+            mom_ref[m : m + 1, :size] += power
             power = power * coord
 
-        lane = lax.broadcasted_iota(jnp.int32, (BLK, LANES), 1).astype(jnp.float32)
-        column = jnp.transpose(jnp.broadcast_to(place, (LANES, BLK)))
+        lane = lax.broadcasted_iota(jnp.int32, (size, LANES), 1).astype(jnp.float32)
+        column = jnp.transpose(jnp.broadcast_to(place, (LANES, size)))
         level = (column - lane) * (1.0 / LANES)
         code = jnp.where(jnp.floor(level) == level, level, -1.0).astype(jnp.bfloat16)
         one = jnp.bfloat16(1.0)
         zero = jnp.bfloat16(0.0)
         for q in range(planes * quads):
-            code_ref[:, q * LANES : (q + 1) * LANES] = jnp.where(code == jnp.bfloat16(q), one, zero).astype(f8)
-
-    def scatter(buffer, fresh):
+            code_ref[:size, q * LANES : (q + 1) * LANES] = jnp.where(code == jnp.bfloat16(q), one, zero).astype(f8)
+
+    grid_refs = (grid0_ref, grid1_ref, grid2_ref)
+
+    def scatter(buffer, size, fresh, ks=tuple(range(TAYLOR))):
         high_ref, low_ref, code_ref = buffer
+        these = pl.ds(ks[0] * per_k, len(ks) * per_k)
         for g in range(groups):
-            hot = code_ref[:, g * 2 * LANES : (g + 1) * 2 * LANES]
-            rest = jnp.dot(low_ref[...], hot, preferred_element_type=jnp.float32)
-            update = jnp.dot(high_ref[...], hot, preferred_element_type=jnp.float32) + rest * (1.0 / low_scale)
-            if fresh:
-                grid_ref[g] = update
-            else:
-                grid_ref[g] += update
-
-    blocks = slots // BLK
+            hot = code_ref[:size, g * 2 * LANES : (g + 1) * 2 * LANES]
+            rest = jnp.dot(low_ref[these, :size], hot, preferred_element_type=jnp.float32)
+            update = jnp.dot(high_ref[these, :size], hot, preferred_element_type=jnp.float32) + rest * (1.0 / low_scale)
+            for i, k in enumerate(ks):
+                piece = update[i * per_k : (i + 1) * per_k]
+                if fresh:
+                    grid_refs[k][g] = piece
+                else:
+                    grid_refs[k][g] += piece
+
     swaps = [
         pltpu.make_async_remote_copy(
             src_ref=source, dst_ref=target, send_sem=pair_send.at[i], recv_sem=pair_recv.at[i],
@@ -305,19 +311,24 @@
         )
         for i, (source, target) in enumerate(((kernel_ref, taps_land), (meta_ref, meta_land)))
     ]
-    order = [(kernel_ref, meta_ref, j) for j in range(blocks)] + [(taps_land, meta_land, j) for j in range(blocks)]
+    own = [(start, BLK) for start in range(0, slots, BLK)]
+    order = [(kernel_ref, meta_ref, piece) for piece in own]
+    order += [(taps_land, meta_land, (start, BLK)) for start in range(0, slots, BLK)]
     prepare(*order[0], buffers[0])
-    for j in range(2 * blocks):
+    for j in range(len(order)):
         if j == 1:
             pl.semaphore_wait(barrier, 1 + n_seat - 1 + n_bl - 1)
             for swap in swaps:
                 swap.start()
-        if j + 1 == blocks:
+        if j + 1 == len(own):
             for swap in swaps:
                 swap.wait()
-        if j + 1 < 2 * blocks:
+        if j + 1 < len(order):
             prepare(*order[j + 1], buffers[(j + 1) % 2])
-        scatter(buffers[j % 2], j == 0)
+        if j + 1 < len(order):
+            scatter(buffers[j % 2], order[j][2][1], j == 0)
+    last = (buffers[(len(order) - 1) % 2], order[-1][2][1], False)
+    scatter(*last, (0, 1))
 
     msend_ref[...] = jnp.broadcast_to(jnp.sum(mom_ref[...], axis=1, keepdims=True), msend_ref.shape)
     def drain(ref, send, recv):
@@ -339,8 +350,9 @@
     ]
 
     def transform(k):
-        low_row = k * per_k
-        pieces = []
+        grid_ref = grid_refs[k]
+        low_row = 0
+        pieces = [[] for b in range(quads)]
         for p in range(planes):
             edges = []
             for b in range(quads):
@@ -358,24 +370,24 @@
                 head_imag = imag[:8] + jnp.where(first, pltpu.roll(edge, held, 0), 0.0)
                 real = jnp.concatenate([head_real, real[8:]], axis=0)
                 imag = jnp.concatenate([head_imag, imag[8:]], axis=0)
-                pieces.append(jnp.concatenate([real, imag], axis=1))
-        high, low = split(jnp.concatenate(pieces, axis=0))
-        spec_ref[k] = (
-            jnp.dot(high, coarse_ref[0], preferred_element_type=jnp.float32)
-            + jnp.dot(high, coarse_ref[1], preferred_element_type=jnp.float32)
-            + jnp.dot(low, coarse_ref[0], preferred_element_type=jnp.float32)
-        )
+                pieces[b].append(jnp.concatenate([real, imag], axis=1))
+        for b in range(quads):
+            high, low = split(jnp.concatenate(pieces[b], axis=0))
+            spec_ref[k, b] = (
+                jnp.dot(high, coarse_ref[b, 0], preferred_element_type=jnp.float32)
+                + jnp.dot(high, coarse_ref[b, 1], preferred_element_type=jnp.float32)
+                + jnp.dot(low, coarse_ref[b, 0], preferred_element_type=jnp.float32)
+            )
 
         def one_plane(p):
             inner = [[None] * pairs for r in range(4)]
             for t in range(pairs):
                 column = []
                 for b in range(quads):
-                    row = pl.ds((p * quads + b) * 32 + t * 8, 8)
-                    x = (spec_ref[k, row, :LANES], spec_ref[k, row, LANES:])
-                    column.append(multiply(x, (twist_ref[0, b, t, 0], twist_ref[0, b, t, 1])))
+                    row = pl.ds(p * 32 + t * 8, 8)
+                    column.append((spec_ref[k, b, row, :LANES], spec_ref[k, b, row, LANES:]))
                 for r, z in enumerate(radix4(column)):
-                    inner[r][t] = multiply(z, (twist_ref[1, r, t, 0], twist_ref[1, r, t, 1])) if r else z
+                    inner[r][t] = multiply(z, (twist_ref[r, t, 0], twist_ref[r, t, 1]))
             for r in range(4):
                 for s, z in enumerate(radix4(inner[r])):
                     if s:
@@ -426,6 +438,8 @@
         send_b(k)
 
     for k in range(TAYLOR):
+        if k == 0:
+            scatter(*last, (2,))
         transform(k)
         send_x(k)
     drain(mxland_ref, xm_send, xm_recv)
@@ -475,7 +489,7 @@
         (tap_table.shape[1:], bf16), (coarse.shape, bf16), (twist.shape, f32), (screen.shape[1:], f32),
         ((8, slots), f32), ((8, slots), f32), (kernel.shape, bf16),
         *block, *block,
-        ((groups, rows_all, 2 * LANES), f32), ((8, BLK), f32), ((TAYLOR, planes * quads * 32, 2 * LANES), f32),
+        ((groups, per_k, 2 * LANES), f32), ((groups, per_k, 2 * LANES), f32), ((groups, per_k, 2 * LANES), f32), ((8, BLK), f32), ((TAYLOR, quads, planes * 32, 2 * LANES), f32),
         ((TAYLOR, 16, 8, LANES), f32), ((LANES, LANES), f32), ((LANES, LANES), f32), ((LANES, LANES), f32),
         ((TAYLOR, n_seat - 1, 2, per * 16, LANES), f32),
         ((TAYLOR, n_bl, share, LANES), f32), ((TAYLOR, n_bl - 1, share, LANES), f32),

time: 23.8 us -> 23.4 us (0.983)
  Pallas kernels: 22.4 us -> 22 us
    pallas_call x1, Pallas kernels: 22.4 us -> 22 us  [strip_image(): pl.pallas_call(functools.partial(strip_kernel, n_chan, n_bl), out_shape=p...]
where the time goes in v5:
time: 23.4 us; the launch traced here: 23.3 us
  Pallas kernels  22 us (94%)
  between operations  0.66 us (3%)
  local copies, waits for them, and re-layouts  0.61 us (3%)
    pallas_call x1, Pallas kernels, strip_image(): pl.pallas_call(functools.partial(strip_kernel, n_chan, n_bl), out_shape=p...  22 us
    unnamed x1, local copies, waits for them, and re-layouts  0.61 us

profile of v5, /device:TPU:0, one launch (start us, length us, event | category | flops | bytes accessed | tf_op | source)
XLA Modules:
  0.0 23.3 jit_solution(3152500608845483400)
XLA Ops:
  0.7 22.0 %strip_image.1 = f32[3,8,128]{2,1,0:T(8,128)S(1)} custom-call(s32[1,1]{1,0:T(1,128)S(6)} %copy.16.count_hbm, f32[1,16]{1,0:T(1,128)} %offset_hbm.1, bf16[2,2048]{1,0:T(2,128)(2,1)} %bitcast.12, bf16[1,2048]{1,0:T(2,128)(2,1)} %bitcast.13, bf16[64,2048]{1,0:T(8,128)(2,1)} %bitcast.11, s32[1,2048]{1,0:T(1,128)} %bitcast.14, s32[1,2048]{1,0:T(1,128)} %bitcast.15, ...), custom_call_target="tpu_custom_call" | custom-call | tf_op jit(solution)/shard_map/strip_image/pallas_call | solution.py:498
  22.7 0.6 %copy.15 = f32[1,3,8,128]{3,1,2,0:T(4,128)} copy(f32[1,3,8,128]{3,2,1,0:T(8,128)S(1)} %bitcast.10) | data formatting | bytes 24576
